TPU v7x, 32 devices: a whole 2x2x4 slice. The times are simulated.
32 devices in a mesh: spin: 2 (over core), band: 8 (over z, x), grid: 2 (over y).
Axes of the slice: x: 2, y: 2, z: 4, core: 2. Of those that a mesh axis runs over, the one named last changes fastest.
Arguments:
- orbitals: bfloat16 [2, 64, 128, 128, 128], P('spin', 'band', 'grid'), may hold values from -0.14941406 to 0.14941406
- partial_bands: int32 [2, 2], P('spin'), may hold values from 0 to 63
- core_density: float32 [128, 128, 128], P('grid'), may hold values from 0.002 to 0.2
Outputs:
- potential: float32 [2, 128, 128, 128], P('spin', 'grid', 'band')
Inputs may be any that keep to these rules, and one draw needn't show every extreme that they name: `partial_bands`: row s holds, for spin s, the first half-occupied band and the count of half-occupied bands; bands past 64 - 1 do not exist.
All inputs are finite; a program needn't handle non-finite values.
Results may differ from a plain program's by a relative error of at most 0.0003.
Values sent between devices are 32-bit elements; how exact they have to be, the bound alone decides.
A program may use at most 128 MiB of HBM per device.

v0:
```python
import functools
import math

import jax
import jax.numpy as jnp
import numpy as np
from jax import lax
from jax.experimental import pallas as pl
from jax.experimental.pallas import tpu as pltpu
from jax.sharding import PartitionSpec as P

KAPPA = 0.804
MU_X = 0.2195149727645171
BETA = 0.06672455060314922
GAMMA = (1.0 - math.log(2.0)) / math.pi**2
FZ_NORM = 2.0 ** (4.0 / 3.0) - 2.0
FPP_ZERO = 1.709921
EXACT = lax.Precision.HIGHEST
MESH = pl.DeviceIdType.MESH
CHUNK = 4
FAST = 2
XC_ROWS = 2
TILE = 8


def cube_root(value):
    return jnp.exp(jnp.log(value) * (1.0 / 3.0))


def pw_fit(radius, root, amp, alpha, beta_one, beta_two, beta_three, beta_four):
    denom = (2.0 * amp) * (
        root * (beta_one + root * (beta_two + root * (beta_three + root * beta_four)))
    )
    return -2.0 * amp * (1.0 + alpha * radius) * jnp.log(1.0 + 1.0 / denom)


def exchange_part(double, sigma_four):
    kfermi = (3.0 * math.pi**2) ** (1.0 / 3.0) * cube_root(double)
    product = kfermi * double
    scaled = sigma_four / (4.0 * product * product)
    enhance = 1.0 + KAPPA - KAPPA / (1.0 + MU_X * scaled / KAPPA)
    return -0.75 / math.pi * product * enhance


def xc_energy(n_up, n_down, s_uu, s_ud, s_dd):
    exch = 0.5 * (exchange_part(2.0 * n_up, 4.0 * s_uu) + exchange_part(2.0 * n_down, 4.0 * s_dd))
    total = n_up + n_down
    zeta = (n_up - n_down) / total
    third = cube_root(total)
    radius = (3.0 / (4.0 * math.pi)) ** (1.0 / 3.0) / third
    root = jnp.sqrt(radius)
    ec_para = pw_fit(radius, root, 0.031091, 0.2137, 7.5957, 3.5876, 1.6382, 0.49294)
    ec_ferro = pw_fit(radius, root, 0.015545, 0.20548, 14.1189, 6.1977, 3.3662, 0.62517)
    neg_stiff = pw_fit(radius, root, 0.016887, 0.11125, 10.357, 3.6231, 0.88026, 0.49671)
    plus_z = 1.0 + zeta
    minus_z = 1.0 - zeta
    plus_third = cube_root(plus_z)
    minus_third = cube_root(minus_z)
    fzeta = (plus_z * plus_third + minus_z * minus_third - 2.0) * (1.0 / FZ_NORM)
    zeta_sq = zeta * zeta
    zeta_four = zeta_sq * zeta_sq
    ec_lda = (
        ec_para
        - neg_stiff * fzeta * (1.0 / FPP_ZERO) * (1.0 - zeta_four)
        + (ec_ferro - ec_para) * fzeta * zeta_four
    )
    phi = 0.5 * (plus_third * plus_third + minus_third * minus_third)
    phi_cube = phi * phi * phi
    kfermi = (3.0 * math.pi**2) ** (1.0 / 3.0) * third
    screen_sq = kfermi * (4.0 / math.pi)
    sigma = s_uu + 2.0 * s_ud + s_dd
    tsq = sigma / (4.0 * phi * phi * screen_sq * total * total)
    amp = BETA / GAMMA / (jnp.exp(-ec_lda / (GAMMA * phi_cube)) - 1.0)
    atsq = amp * tsq
    gradient_term = (
        GAMMA
        * phi_cube
        * jnp.log(1.0 + BETA / GAMMA * tsq * (1.0 + atsq) / (1.0 + atsq + atsq * atsq))
    )
    return exch + total * (ec_lda + gradient_term)


def spectral_table(length):
    index = np.arange(length)
    angle = 2.0 * np.pi / length * (index[:, None] * index[None, :] % length)
    mode = np.where(index < length // 2, index, index - length)
    mode = np.where(index == length // 2, 0, mode)
    wave = 2.0 * np.pi / length * mode
    sines, cosines = np.sin(angle), np.cos(angle)
    first_term = (sines * wave[None, :]) @ cosines.T
    second_term = (cosines * wave[None, :]) @ sines.T
    return ((second_term - first_term) / length).astype(np.float32)


def potential_kernel(
    bands,
    grids,
    pairs_ref,
    orb_hbm,
    core_hbm,
    tx_ref,
    ty_ref,
    tz_ref,
    out_ref,
    orb,
    core,
    part,
    x_in,
    z_out,
    p_in,
    w_out,
    w_in,
    own,
    line,
    gx,
    hx,
    sx,
    gy,
    hy,
    sy,
    dx,
    dz,
    other,
    fields,
    outgoing,
    orb_sem,
    core_sem,
    x_send,
    x_recv,
    p_send,
    p_recv,
    w_send,
    w_recv,
    xp_send,
    xp_recv,
    xf_send,
    xf_recv,
    xb_send,
    xb_recv,
    yf_send,
    yf_recv,
    yb_send,
    yb_recv,
    in_send,
    in_recv,
    gy_send,
    gy_recv,
    out_send,
    out_recv,
):
    count, rows, y_cells, z_cells = orb.shape
    block = core.shape[1]
    slow = bands // FAST
    steps = out_send.shape[0]
    r_part = rows // bands
    chunk = r_part // steps
    piece_rows = rows // xp_send.shape[0]
    pieces = rows // piece_rows
    per_piece = piece_rows // chunk
    chunks = rows // chunk
    y_part = block // grids
    half = bands // 2
    xc_rows = math.gcd(XC_ROWS, chunk)
    me = lax.axis_index("band")
    slab = lax.axis_index("grid")
    spin = lax.axis_index("spin")
    my_slow, my_fast = lax.div(me, FAST), lax.rem(me, FAST)
    partner = {"band": my_slow * FAST + (1 - my_fast)}
    pairs = slow // 2
    my_pair = lax.div(my_slow, 2)
    my_kind = lax.rem(my_slow + my_pair, 2)
    beside = {"band": (my_slow + 1 - 2 * lax.rem(my_slow, 2)) * FAST + my_fast}
    twin = {"spin": 1 - spin}
    my_block = pl.ds(pl.multiple_of(me * block, TILE), block)
    my_slab = pl.ds(pl.multiple_of(slab * rows, TILE), rows)
    mine = pl.ds(spin * half, half)
    theirs = pl.ds((1 - spin) * half, half)

    def remote(src, dst, send, recv, device):
        return pltpu.make_async_remote_copy(
            src_ref=src,
            dst_ref=dst,
            send_sem=send,
            recv_sem=recv,
            device_id=device,
            device_id_type=MESH,
        )

    def orb_copy(u):
        span = pl.ds(u * piece_rows, piece_rows)
        return pltpu.make_async_copy(orb_hbm.at[0, :, span], orb.at[:, span], orb_sem.at[u])

    def core_copy():
        return pltpu.make_async_copy(core_hbm.at[:, my_block], core, core_sem)

    def x_copy(c):
        span = pl.ds(c * chunk, chunk)
        return remote(
            part.at[1 - my_fast, span], x_in.at[span], x_send.at[c], x_recv.at[c], partner
        )

    def pair_copy(c):
        span = pl.ds(c * chunk, chunk)
        return remote(
            z_out.at[1 - my_kind, :, span],
            p_in.at[:, span],
            p_send.at[c],
            p_recv.at[c],
            beside,
        )

    def z_copy(c, k):
        span = pl.ds(c * chunk, chunk)
        h = lax.rem(my_pair + k, pairs)
        return remote(
            w_out.at[h, span],
            w_in.at[k - 1, span],
            w_send.at[k - 1, c],
            w_recv.at[k - 1, c],
            {"band": (2 * h + lax.rem(my_kind + h, 2)) * FAST + my_fast},
        )

    def x_piece(u, k):
        q = lax.rem(slab + k, grids)
        start = pl.multiple_of(u * piece_rows, TILE)
        there = pl.multiple_of(slab * rows + u * piece_rows, TILE)
        return remote(
            line.at[0, pl.ds(q * y_part, y_part), pl.ds(start, piece_rows)],
            gx.at[0, :, pl.ds(there, piece_rows)],
            xp_send.at[u, k - 1],
            xp_recv.at[u, k - 1],
            {"grid": q},
        )

    def x_whole(k):
        q = lax.rem(slab + k, grids)
        return remote(
            line.at[1, pl.ds(q * y_part, y_part)],
            gx.at[1, :, my_slab],
            xf_send.at[k - 1],
            xf_recv.at[k - 1],
            {"grid": q},
        )

    def x_back(t, k):
        q = lax.rem(slab + k, grids)
        return remote(
            hx.at[t, :, pl.ds(pl.multiple_of(q * rows, TILE), rows)],
            sx.at[t, pl.ds(slab * y_part, y_part)],
            xb_send.at[t, k - 1],
            xb_recv.at[t, k - 1],
            {"grid": q},
        )

    def y_forward(t, s, k):
        q = lax.rem(me + k, bands)
        source = own if t == 0 else fields.at[2]
        return remote(
            source.at[q, pl.ds(s * chunk, chunk)],
            gy.at[t, pl.ds(s * chunk, chunk), my_block],
            yf_send.at[t, s, k - 1],
            yf_recv.at[t, s, k - 1],
            {"band": q},
        )

    def y_back(t, s, k):
        q = lax.rem(me + k, bands)
        return remote(
            hy.at[t, pl.ds(s * chunk, chunk), pl.ds(pl.multiple_of(q * block, TILE), block)],
            sy.at[t, me, pl.ds(s * chunk, chunk)],
            yb_send.at[t, s, k - 1],
            yb_recv.at[t, s, k - 1],
            {"band": q},
        )

    incoming = [own, dz, dx]

    def swap_in(f):
        return remote(incoming[f].at[theirs], other.at[f], in_send.at[f], in_recv.at[f], twin)

    def swap_steep(s):
        span = pl.ds(s * chunk, chunk)
        return remote(
            sy.at[0, theirs, span], other.at[3, :, span], gy_send.at[s], gy_recv.at[s], twin
        )

    def swap_out(s):
        span = pl.ds(s * chunk, chunk)
        return remote(
            outgoing.at[:, :, span],
            fields.at[:, mine, span],
            out_send.at[s],
            out_recv.at[s],
            twin,
        )

    def times(table, field):
        return jnp.dot(table, field, precision=EXACT, preferred_element_type=jnp.float32)

    def turned(value):
        return jnp.transpose(value, (1, 0, 2))

    def whole(value):
        return value.reshape(rows, block, z_cells)

    def split(value):
        return value.reshape(bands, r_part, block, z_cells)

    def along_third(field):
        return times(field.reshape(rows * block, z_cells), tz_ref[...]).reshape(field.shape)

    def along_first(t):
        for y in range(y_part):
            hx[t, y] = times(tx_ref[...], gx[t, y])
        for k in range(1, grids):
            x_back(t, k).start()
        sx[t, pl.ds(slab * y_part, y_part)] = hx[t, :, my_slab]

    def along_second(t, s):
        for k in range(1, bands):
            y_forward(t, s, k).wait_recv()
        for r in range(s * chunk, (s + 1) * chunk):
            hy[t, r] = times(ty_ref[...], gy[t, r])
        for k in range(1, bands):
            y_back(t, s, k).start()
        span = pl.ds(s * chunk, chunk)
        sy[t, me, span] = hy[t, span, my_block]

    def end_first(t):
        for k in range(1, grids):
            x_back(t, k).wait_recv()
        return split(turned(sx[t]))

    def end_second(t, s):
        for k in range(1, bands):
            y_back(t, s, k).wait_recv()

    def each(number, body):
        lax.fori_loop(0, number, lambda i, carry: (body(i), carry)[1], 0)

    def order(u):
        if pieces != bands:
            return u
        v, fast = u % slow, u // slow
        late = v // pairs
        return (v + late * (pairs + slow - 1 - 2 * v)) * FAST + fast

    each(pieces, lambda u: orb_copy(order(u)).start())
    core_copy().start()
    partners = (
        [twin]
        + [{"grid": lax.rem(slab + k, grids)} for k in range(1, grids)]
        + [{"band": lax.rem(me + k, bands)} for k in range(1, bands)]
    )
    barrier = pltpu.get_barrier_semaphore()
    for target in partners:
        pl.semaphore_signal(barrier, inc=1, device_id=target, device_id_type=MESH)
    first = pairs_ref[0, 0]
    last = first + pairs_ref[0, 1]
    weights = []
    for n in range(count):
        ident = me * count + n
        weights.append(jnp.where((ident >= first) & (ident < last), 0.5, 1.0).astype(jnp.float32))

    def squares(u):
        orb_copy(u).wait()

        def one_chunk(i):
            c = u * per_piece + i
            for r in range(chunk):
                row = c * chunk + r
                for b in range(bands):
                    total = jnp.zeros((block, z_cells), jnp.float32)
                    for n in range(count):
                        values = orb[n, row, b * block : (b + 1) * block].astype(jnp.float32)
                        total += weights[n] * (values * values)
                    part[b % FAST, row, b // FAST] = total

        each(per_piece, one_chunk)

    def send_squares(u):
        each(per_piece, lambda i: x_copy(u * per_piece + i).start())

    def forward(u):
        def one_chunk(i):
            c = u * per_piece + i
            x_copy(c).wait_recv()
            span = pl.ds(c * chunk, chunk)
            for d in range(slow):
                z_out[(d + d // 2) % 2, d // 2, span] = part[my_fast, span, d] + x_in[span, d]
            pair_copy(c).start()

        each(per_piece, one_chunk)

    def join(u):
        def one_chunk(i):
            c = u * per_piece + i
            pair_copy(c).wait_recv()
            span = pl.ds(c * chunk, chunk)
            w_out[:, span] = z_out[my_kind, :, span] + p_in[:, span]
            for k in range(1, pairs):
                z_copy(c, k).start()

        each(per_piece, one_chunk)

    def collect(u):
        def one_chunk(i):
            c = u * per_piece + i
            span = pl.ds(c * chunk, chunk)
            total = 0.5 * core[span] + w_out[my_pair, span]
            for k in range(1, pairs):
                z_copy(c, k).wait_recv()
                total += w_in[k - 1, span]
            j, s = lax.div(c, steps), lax.rem(c, steps)
            own[j, pl.ds(s * chunk, chunk)] = total

            @pl.when(j != me)
            def _():
                y_forward(0, s, lax.rem(j - me + bands, bands)).start()

            @pl.when(j == me)
            def _():
                gy[0, pl.ds(s * chunk, chunk), my_block] = total

        each(per_piece, one_chunk)
        group = piece_rows // r_part
        rows_here = own[pl.ds(u * group, group)].reshape(piece_rows, block, z_cells)
        start = pl.multiple_of(u * piece_rows, TILE)
        there = pl.multiple_of(slab * rows + u * piece_rows, TILE)
        line[0, :, pl.ds(start, piece_rows)] = turned(rows_here)
        for k in range(1, grids):
            x_piece(u, k).start()
        gx[0, :, pl.ds(there, piece_rows)] = line[
            0, pl.ds(slab * y_part, y_part), pl.ds(start, piece_rows)
        ]

    squares(order(0))
    squares(order(1))
    pl.semaphore_wait(barrier, len(partners))
    send_squares(order(0))
    send_squares(order(1))
    core_copy().wait()

    def sum_step(u):
        forward(order(u))

        @pl.when(u + 2 < pieces)
        def _():
            squares(order(u + 2))
            send_squares(order(u + 2))

        @pl.when(u >= 1)
        def _():
            join(order(u - 1))

        @pl.when(u >= 2)
        def _():
            collect(order(u - 2))

    each(pieces, sum_step)
    join(order(pieces - 1))
    collect(order(pieces - 2))
    collect(order(pieces - 1))

    swap_in(0).start()
    dz[...] = along_third(own[...])
    swap_in(1).start()
    along_second(0, 0)
    for u in range(pieces):
        for k in range(1, grids):
            x_piece(u, k).wait_recv()
    along_first(0)
    for s in range(1, steps):
        along_second(0, s)
    dx[...] = end_first(0)
    swap_in(2).start()
    for f in range(3):
        swap_in(f).wait()

    def potential_rows(j, row):
        span = pl.ds(row, xc_rows)
        here = (spin * half + j, span)
        there = (j, span)
        n_own, n_other = own[here], other[(0,) + there]
        g_own = [dx[here], sy[(0,) + here], dz[here]]
        g_other = [other[(2,) + there], other[(3,) + there], other[(1,) + there]]
        s_own = g_own[0] * g_own[0] + g_own[1] * g_own[1] + g_own[2] * g_own[2]
        s_mix = g_own[0] * g_other[0] + g_own[1] * g_other[1] + g_own[2] * g_other[2]
        s_other = g_other[0] * g_other[0] + g_other[1] * g_other[1] + g_other[2] * g_other[2]
        energy, pull = jax.vjp(xc_energy, n_own, n_other, s_own, s_mix, s_other)
        derivs = pull(jnp.ones_like(energy))
        fields[(0,) + here] = derivs[0]
        outgoing[(0,) + there] = derivs[1]
        for a in range(3):
            fields[(1 + a,) + here] = 2.0 * derivs[2] * g_own[a] + derivs[3] * g_other[a]
            outgoing[(1 + a,) + there] = 2.0 * derivs[4] * g_other[a] + derivs[3] * g_own[a]

    def flux_out(s):
        swap_out(s).wait_recv()
        for k in range(1, bands):
            y_forward(1, s, k).start()
        span = pl.ds(s * chunk, chunk)
        gy[1, span, my_block] = fields[2, me, span]

    end_second(0, 0)
    swap_steep(0).start()
    for s in range(steps):
        swap_steep(s).wait_recv()
        per_group = chunk // xc_rows
        each(
            half * per_group,
            lambda i: potential_rows(
                lax.div(i, per_group), s * chunk + lax.rem(i, per_group) * xc_rows
            ),
        )
        swap_out(s).start()
        if s + 1 < steps:
            end_second(0, s + 1)
            swap_steep(s + 1).start()
        flux_out(s)

    line[1] = turned(whole(fields[1]))
    for k in range(1, grids):
        x_whole(k).start()
    gx[1, :, my_slab] = line[1, pl.ds(slab * y_part, y_part)]
    for s in range(steps - 1):
        along_second(1, s)
    dz[...] = fields[0] - along_third(fields[3])
    for k in range(1, grids):
        x_whole(k).wait_recv()
    along_first(1)
    along_second(1, steps - 1)
    dz[...] = dz[...] - end_first(1)
    for s in range(steps):
        end_second(1, s)
    out_ref[...] = whole(dz[...] - sy[1])

    def drain(c):
        x_copy(c).wait_send()
        pair_copy(c).wait_send()
        for k in range(1, pairs):
            z_copy(c, k).wait_send()

    each(chunks, drain)
    for k in range(1, grids):
        for u in range(pieces):
            x_piece(u, k).wait_send()
        x_whole(k).wait_send()
        x_back(0, k).wait_send()
        x_back(1, k).wait_send()
    for t in range(2):
        for s in range(steps):
            for k in range(1, bands):
                y_forward(t, s, k).wait_send()
                y_back(t, s, k).wait_send()
    for s in range(steps):
        swap_steep(s).wait_send()
        swap_out(s).wait_send()


def potential_call(orbitals, partial_bands, core_density, tables):
    bands, grids = lax.axis_size("band"), lax.axis_size("grid")
    _, count, rows, y_cells, z_cells = orbitals.shape
    block, slow = y_cells // bands, bands // FAST
    y_part, r_part = block // grids, rows // bands
    x_cells = rows * grids
    steps = r_part // math.gcd(CHUNK, r_part)
    chunks = bands * steps
    pieces = rows // max(r_part, TILE)
    half = bands // 2
    vmem = pl.BlockSpec(memory_space=pltpu.VMEM)
    hbm = pl.BlockSpec(memory_space=pl.ANY)
    dma = pltpu.SemaphoreType.DMA
    real = jnp.float32
    cells = (bands, r_part, block, z_cells)
    return pl.pallas_call(
        functools.partial(potential_kernel, bands, grids),
        out_shape=jax.ShapeDtypeStruct((rows, block, z_cells), real),
        in_specs=[pl.BlockSpec(memory_space=pltpu.SMEM), hbm, hbm] + [vmem] * 3,
        out_specs=vmem,
        scratch_shapes=[
            pltpu.VMEM((count, rows, y_cells, z_cells), jnp.bfloat16),
            pltpu.VMEM((rows, block, z_cells), real),
            pltpu.VMEM((FAST, rows, slow, block, z_cells), real),
            pltpu.VMEM((rows, slow, block, z_cells), real),
            pltpu.VMEM((2, slow // 2, rows, block, z_cells), real),
            pltpu.VMEM((slow // 2, rows, block, z_cells), real),
            pltpu.VMEM((slow // 2, rows, block, z_cells), real),
            pltpu.VMEM((slow // 2 - 1, rows, block, z_cells), real),
            pltpu.VMEM(cells, real),
            pltpu.VMEM((2, block, rows, z_cells), real),
            pltpu.VMEM((2, y_part, x_cells, z_cells), real),
            pltpu.VMEM((2, y_part, x_cells, z_cells), real),
            pltpu.VMEM((2, block, rows, z_cells), real),
            pltpu.VMEM((2, r_part, y_cells, z_cells), real),
            pltpu.VMEM((2, r_part, y_cells, z_cells), real),
            pltpu.VMEM((2,) + cells, real),
            pltpu.VMEM(cells, real),
            pltpu.VMEM(cells, real),
            pltpu.VMEM((4, half) + cells[1:], real),
            pltpu.VMEM((4,) + cells, real),
            pltpu.VMEM((4, half) + cells[1:], real),
            dma((pieces,)),
            dma,
            dma((chunks,)),
            dma((chunks,)),
            dma((chunks,)),
            dma((chunks,)),
            dma((slow // 2 - 1, chunks)),
            dma((slow // 2 - 1, chunks)),
        ]
        + [dma((pieces, grids - 1))] * 2
        + [dma((grids - 1,))] * 2
        + [dma((2, grids - 1))] * 2
        + [dma((2, steps, bands - 1))] * 4
        + [dma((3,))] * 2
        + [dma((steps,))] * 4,
        compiler_params=pltpu.CompilerParams(
            collective_id=0, has_side_effects=True, vmem_limit_bytes=60 * 2**20
        ),
        name="potential",
    )(partial_bands, orbitals, core_density, *tables)


def per_device(orbitals, partial_bands, core_density):
    x_rows, y_cols, z_cells = core_density.shape
    tables = (
        jnp.asarray(spectral_table(x_rows * lax.axis_size("grid"))),
        jnp.asarray(spectral_table(y_cols)),
        jnp.asarray(spectral_table(z_cells).T),
    )
    return potential_call(orbitals, partial_bands, core_density, tables)[None]


def solution(mesh):
    in_specs = (P("spin", "band", "grid", None, None), P("spin", None), P("grid", None, None))
    out_specs = P("spin", "grid", "band", None)
    return jax.shard_map(
        per_device, mesh=mesh, in_specs=in_specs, out_specs=out_specs, check_vma=False
    )
```

profile of v0, /device:TPU:0, one launch (start us, length us, event | category | flops | bytes accessed | tf_op | source)
XLA Modules:
  0.0 114.6 jit_solution(1594545357200207076)
XLA Ops:
  0.0 112.7 %potential.1 = f32[64,16,128]{2,1,0:T(8,128)} custom-call(s32[1,2]{1,0:T(1,128)} %pairs_ref.1, bf16[1,8,64,128,128]{4,3,2,1,0:T(8,128)(2,1)} %orb_hbm.1, f32[64,128,128]{2,1,0:T(8,128)} %core_hbm.1, f32[128,128]{1,0:T(8,128)} %constant.4.clone.tx_ref.ty_ref, f32[128,128]{1,0:T(8,128)} %constant.4.clone.tx_ref.ty_ref, f32[128,128]{1,0:T(8,128)} %constant.5.clone.tz_ref), custom_call_target="tpu_custom_call" | custom-call | tf_op jit(solution)/shard_map/potential/pallas_call | solution.py:576
  112.7 1.9 %copy.8 = f32[1,64,16,128]{3,2,1,0:T(8,128)} copy(f32[1,64,16,128]{3,2,1,0:T(8,128)} %bitcast.1) | data formatting | bytes 1048576
where the time goes:
time: 115 us
  Pallas kernels  113 us (98%)
  local copies, waits for them, and re-layouts  1.87 us (2%)
    pallas_call x1, Pallas kernels, potential_call(): pl.pallas_call(functools.partial(potential_kernel, bands, grids), out_sha...  113 us

commit v1 on v0

v1 whole, which is shorter than its diff:
```python
import functools
import math

import jax
import jax.numpy as jnp
import numpy as np
from jax import lax
from jax.experimental import pallas as pl
from jax.experimental.pallas import tpu as pltpu
from jax.sharding import PartitionSpec as P

KAPPA = 0.804
MU_X = 0.2195149727645171
BETA = 0.06672455060314922
GAMMA = (1.0 - math.log(2.0)) / math.pi**2
FZ_NORM = 2.0 ** (4.0 / 3.0) - 2.0
FPP_ZERO = 1.709921
MESH = pl.DeviceIdType.MESH
CHUNK = 4
AHEAD = 3
LATE = 2
FAST = 2
XC_ROWS = 2
TILE = 8


def cube_root(value):
    return jnp.exp(jnp.log(value) * (1.0 / 3.0))


def pw_fit(radius, root, amp, alpha, beta_one, beta_two, beta_three, beta_four):
    denom = (2.0 * amp) * (
        root * (beta_one + root * (beta_two + root * (beta_three + root * beta_four)))
    )
    return -2.0 * amp * (1.0 + alpha * radius) * jnp.log(1.0 + 1.0 / denom)


def exchange_part(double, sigma_four):
    kfermi = (3.0 * math.pi**2) ** (1.0 / 3.0) * cube_root(double)
    product = kfermi * double
    scaled = sigma_four / (4.0 * product * product)
    enhance = 1.0 + KAPPA - KAPPA / (1.0 + MU_X * scaled / KAPPA)
    return -0.75 / math.pi * product * enhance


def xc_energy(n_up, n_down, s_uu, s_ud, s_dd):
    exch = 0.5 * (exchange_part(2.0 * n_up, 4.0 * s_uu) + exchange_part(2.0 * n_down, 4.0 * s_dd))
    total = n_up + n_down
    zeta = (n_up - n_down) / total
    third = cube_root(total)
    radius = (3.0 / (4.0 * math.pi)) ** (1.0 / 3.0) / third
    root = jnp.sqrt(radius)
    ec_para = pw_fit(radius, root, 0.031091, 0.2137, 7.5957, 3.5876, 1.6382, 0.49294)
    ec_ferro = pw_fit(radius, root, 0.015545, 0.20548, 14.1189, 6.1977, 3.3662, 0.62517)
    neg_stiff = pw_fit(radius, root, 0.016887, 0.11125, 10.357, 3.6231, 0.88026, 0.49671)
    plus_z = 1.0 + zeta
    minus_z = 1.0 - zeta
    plus_third = cube_root(plus_z)
    minus_third = cube_root(minus_z)
    fzeta = (plus_z * plus_third + minus_z * minus_third - 2.0) * (1.0 / FZ_NORM)
    zeta_sq = zeta * zeta
    zeta_four = zeta_sq * zeta_sq
    ec_lda = (
        ec_para
        - neg_stiff * fzeta * (1.0 / FPP_ZERO) * (1.0 - zeta_four)
        + (ec_ferro - ec_para) * fzeta * zeta_four
    )
    phi = 0.5 * (plus_third * plus_third + minus_third * minus_third)
    phi_cube = phi * phi * phi
    kfermi = (3.0 * math.pi**2) ** (1.0 / 3.0) * third
    screen_sq = kfermi * (4.0 / math.pi)
    sigma = s_uu + 2.0 * s_ud + s_dd
    tsq = sigma / (4.0 * phi * phi * screen_sq * total * total)
    amp = BETA / GAMMA / (jnp.exp(-ec_lda / (GAMMA * phi_cube)) - 1.0)
    atsq = amp * tsq
    gradient_term = (
        GAMMA
        * phi_cube
        * jnp.log(1.0 + BETA / GAMMA * tsq * (1.0 + atsq) / (1.0 + atsq + atsq * atsq))
    )
    return exch + total * (ec_lda + gradient_term)


def spectral_table(length):
    index = np.arange(length)
    angle = 2.0 * np.pi / length * (index[:, None] * index[None, :] % length)
    mode = np.where(index < length // 2, index, index - length)
    mode = np.where(index == length // 2, 0, mode)
    wave = 2.0 * np.pi / length * mode
    sines, cosines = np.sin(angle), np.cos(angle)
    first_term = (sines * wave[None, :]) @ cosines.T
    second_term = (cosines * wave[None, :]) @ sines.T
    return (second_term - first_term) / length


def halves_of_table(table):
    high = table.astype(jnp.bfloat16)
    low = (table - high.astype(np.float64)).astype(jnp.bfloat16)
    return high, low


def left_table(table):
    high, low = halves_of_table(table)
    return np.concatenate([np.concatenate([part, part], axis=1) for part in (high, low)], axis=0)


def right_table(table):
    high, low = halves_of_table(table)
    both = np.concatenate([high, low], axis=1)
    return np.concatenate([both, both], axis=0)


def halves(field):
    high = field.astype(jnp.bfloat16)
    return high, (field - high.astype(jnp.float32)).astype(jnp.bfloat16)


def from_left(table, field):
    product = jnp.dot(
        table, jnp.concatenate(halves(field), axis=0), preferred_element_type=jnp.float32
    )
    rows = product.shape[0] // 2
    return product[:rows] + product[rows:]


def from_right(field, table):
    product = jnp.dot(
        jnp.concatenate(halves(field), axis=1), table, preferred_element_type=jnp.float32
    )
    columns = product.shape[1] // 2
    return product[:, :columns] + product[:, columns:]


def potential_kernel(
    bands,
    grids,
    pairs_ref,
    orb_hbm,
    core_hbm,
    tx_ref,
    ty_ref,
    tz_ref,
    out_ref,
    orb,
    core,
    part,
    x_in,
    z_out,
    z_in,
    own,
    gx,
    hx,
    nx,
    gy,
    hy,
    ny,
    dz,
    n_twin,
    nx_twin,
    fx,
    fx_out,
    fy,
    fz,
    s_out,
    base,
    sy,
    orb_sem,
    core_sem,
    x_send,
    x_recv,
    z_send,
    z_recv,
    g_send,
    g_recv,
    n_send,
    n_recv,
    nx_send,
    nx_recv,
    yf_send,
    yf_recv,
    yb_send,
    yb_twin,
    yb_recv,
    fy_send,
    fy_other,
    fy_recv,
    fx_send,
    fx_recv,
    s_send,
    s_recv,
    sb_send,
    sb_recv,
):
    count, rows, y_cells, z_cells = orb.shape
    block = core.shape[1]
    slow = bands // FAST
    chunk = x_in.shape[1] // x_recv.shape[0]
    chunks = rows // chunk
    per_unit = TILE // chunk
    units = rows // (2 * TILE)
    groups = rows // bands
    per_group = bands // chunk
    pair_groups = 2 * TILE // bands
    me = lax.axis_index("band")
    slab = lax.axis_index("grid")
    spin = lax.axis_index("spin")
    place, fast = lax.div(me, FAST), lax.rem(me, FAST)
    across = {"band": place * FAST + (1 - fast)}
    twin = {"spin": 1 - spin}
    my_block = pl.ds(pl.multiple_of(me * block, TILE), block)

    def remote(src, dst, send, recv, device):
        return pltpu.make_async_remote_copy(
            src_ref=src,
            dst_ref=dst,
            send_sem=send,
            recv_sem=recv,
            device_id=device,
            device_id_type=MESH,
        )

    def take(ref, sem):
        pltpu.make_async_copy(ref, ref, sem).wait()

    def each(number, body):
        lax.fori_loop(0, number, lambda i, carry: (body(i), carry)[1], 0)

    def chunk_span(c):
        return pl.ds(c * chunk, chunk)

    def unit_rows(w):
        return pl.ds(pl.multiple_of(w * TILE, TILE), TILE)

    def line_rows(w):
        return pl.ds(pl.multiple_of(slab * rows + w * TILE, TILE), TILE)

    def band_block(j):
        return pl.ds(pl.multiple_of(j * block, TILE), block)

    def turned(value):
        return jnp.transpose(value, (1, 0, 2))

    def orb_copy(c):
        span = chunk_span(c)
        return pltpu.make_async_copy(orb_hbm.at[0, :, span], orb.at[:, span], orb_sem.at[c])

    def core_copy():
        return pltpu.make_async_copy(core_hbm.at[:, my_block], core, core_sem)

    def x_copy(c):
        span = chunk_span(c)
        return remote(part.at[1 - fast, :, span], x_in.at[:, span], x_send, x_recv.at[c], across)

    def z_copy(c, d, slot, to):
        span = chunk_span(c)
        return remote(
            z_out.at[d, span],
            z_in.at[slot, span],
            z_send,
            z_recv.at[c, slot],
            {"band": to * FAST + fast},
        )

    def gather_copy(w, k):
        return remote(
            gx.at[0, :, line_rows(w)],
            gx.at[0, :, line_rows(w)],
            g_send.at[w, k - 1],
            g_recv.at[w, k - 1],
            {"grid": lax.rem(slab + k, grids)},
        )

    def n_copy(v):
        return remote(
            own.at[unit_rows(2 * v + 1 - spin)], n_twin.at[v], n_send.at[v], n_recv.at[v], twin
        )

    def nx_copy(v):
        return remote(
            nx.at[unit_rows(2 * v + 1 - spin)], nx_twin.at[v], nx_send.at[v], nx_recv.at[v], twin
        )

    def fx_same(v, k):
        return remote(
            gx.at[1, :, line_rows(2 * v + spin)],
            gx.at[1, :, line_rows(2 * v + spin)],
            fx_send.at[0, v, k],
            fx_recv.at[0, v, k],
            {"grid": lax.rem(slab + k, grids)},
        )

    def fx_cross(v, k):
        return remote(
            fx_out.at[v],
            gx.at[1, :, line_rows(2 * v + spin)],
            fx_send.at[1, v, k],
            fx_recv.at[1, v, k],
            {"spin": 1 - spin, "grid": lax.rem(slab + k, grids)},
        )

    def s_copy(v):
        return remote(
            s_out.at[v], base.at[unit_rows(2 * v + spin)], s_send.at[v], s_recv.at[v], twin
        )

    def my_row(i):
        row = i * bands + me
        unit = lax.div(row, TILE)
        return row, lax.rem(unit, 2), lax.div(unit, 2), lax.rem(row, TILE)

    def yb_copy(i, j, send):
        row, holder, v, e = my_row(i)
        slot = jnp.where(holder == spin, 0, 1)
        return remote(
            hy.at[0, i, band_block(j)],
            ny.at[slot, v, e],
            send,
            yb_recv.at[slot, v, e],
            {"spin": holder, "band": j},
        )

    def fy_own(v, e, i, q):
        return remote(
            fy.at[0, v, e],
            gy.at[1, i, my_block],
            fy_send.at[v, e],
            fy_recv.at[i, 0],
            {"band": q},
        )

    def fy_cross(v, e, i, q):
        return remote(
            fy.at[1, v, e],
            gy.at[1, i, my_block],
            fy_other,
            fy_recv.at[i, jnp.where(q == me, 1, 0)],
            {"spin": 1 - spin, "band": q},
        )

    def sb_copy(i, k):
        q = lax.rem(me + k, bands)
        return remote(
            hy.at[1, i, band_block(q)],
            sy.at[i * bands + me],
            sb_send,
            sb_recv.at[i],
            {"band": q},
        )

    each(chunks, lambda c: orb_copy(c).start())
    core_copy().start()
    barrier = pltpu.get_barrier_semaphore()
    partners = [{"spin": 1 - spin}]
    for core_id in (spin, 1 - spin):
        partners += [{"spin": core_id, "band": lax.rem(me + k, bands)} for k in range(1, bands)]
        partners += [{"spin": core_id, "grid": lax.rem(slab + k, grids)} for k in range(1, grids)]
    for target in partners:
        pl.semaphore_signal(barrier, inc=1, device_id=target, device_id_type=MESH)
    first = pairs_ref[0, 0]
    last = first + pairs_ref[0, 1]
    weights = []
    for n in range(count):
        ident = me * count + n
        weights.append(jnp.where((ident >= first) & (ident < last), 0.5, 1.0).astype(jnp.float32))

    def squares(c):
        orb_copy(c).wait()
        for r in range(chunk):
            row = c * chunk + r
            for b in range(bands):
                total = jnp.zeros((block, z_cells), jnp.float32)
                for n in range(count):
                    values = orb[n, row, b * block : (b + 1) * block].astype(jnp.float32)
                    total += weights[n] * (values * values)
                part[b % FAST, b // FAST, row] = total

    def sum_across(c):
        x_copy(c).wait_recv()
        span = chunk_span(c)
        for d in range(slow):
            z_out[d, span] = part[fast, d, span] + x_in[d, span]

        @pl.when(place == 0)
        def _():
            for d in range(slow - 1, 0, -1):
                z_copy(c, d, d, 1).start()

        @pl.when(place == slow - 1)
        def _():
            for d in range(slow - 1):
                z_copy(c, d, slow if d == slow - 2 else d, slow - 2).start()

    def hop(h, c):
        span = chunk_span(c)

        @pl.when(place == h)
        def _():
            for d in range(slow - 1, h - 1, -1):
                z_copy(c, d, d, h).wait_recv()
                z_out[d, span] += z_in[d, span]
                if d > h:
                    z_copy(c, d, d, h + 1).start()

        at = slow - 1 - h

        @pl.when(place == at)
        def _():
            for d in range(at + 1):
                slot = slow if d == at else d
                z_copy(c, d, slot, at).wait_recv()
                z_out[d, span] += z_in[slot, span]
                if d < at:
                    z_copy(c, d, slow if d == at - 1 else d, at - 1).start()

    def collect(c):
        span = chunk_span(c)
        own[span] = 0.5 * core[span] + z_out[place, span]
        for r in range(chunk):
            row = c * chunk + r
            i, q = lax.div(row, bands), lax.rem(row, bands)

            @pl.when(q != me)
            def _():
                remote(
                    own.at[row], gy.at[0, i, my_block], yf_send, yf_recv.at[i], {"band": q}
                ).start()

            @pl.when(q == me)
            def _():
                gy[0, i, my_block] = own[row]

    def share(w):
        v = lax.div(w, 2)
        gx[0, :, line_rows(w)] = turned(own[unit_rows(w)])
        for k in range(1, grids):
            gather_copy(w, k).start()

        @pl.when(lax.rem(w, 2) != spin)
        def _():
            n_copy(v).start()

        @pl.when(lax.rem(w, 2) == spin)
        def _():
            field = own[unit_rows(w)].reshape(TILE * block, z_cells)
            dz[0, v] = from_right(field, tz_ref[...]).reshape(TILE, block, z_cells)

    def steep_second(i):
        take(gy.at[0, i, pl.ds(0, (bands - 1) * block)], yf_recv.at[i])
        hy[0, i] = from_left(ty_ref[...], gy[0, i])
        for k in range(1, bands):
            yb_copy(i, lax.rem(me + k, bands), yb_send).start()
        row, holder, v, e = my_row(i)

        @pl.when(holder == spin)
        def _():
            ny[0, v, e] = hy[0, i, my_block]

        @pl.when(holder != spin)
        def _():
            yb_copy(i, me, yb_twin.at[i]).start()

    def along_first(t):
        table = tx_ref[slab]
        for y in range(0, block, 2):
            pair = jnp.concatenate([gx[t, y], gx[t, y + 1]], axis=1)
            product = from_left(table, pair)
            hx[y] = product[:, :z_cells]
            hx[y + 1] = product[:, z_cells:]

    ahead = min(AHEAD, chunks)
    for c in range(ahead):
        squares(c)
        if c == 0:
            pl.semaphore_wait(barrier, len(partners))
        x_copy(c).start()
    core_copy().wait()
    end = chunks + slow - 1 + LATE

    def step(u):
        @pl.when(u + ahead < chunks)
        def _():
            squares(u + ahead)
            x_copy(u + ahead).start()

        @pl.when(u < chunks)
        def _():
            sum_across(u)

        for h in range(1, slow):

            @pl.when((u >= h) & (u < chunks + h))
            def _():
                hop(h, u - h)

        done = u - (slow - 1)

        @pl.when((done >= 0) & (done < chunks))
        def _():
            collect(done)

            @pl.when(lax.rem(done, per_unit) == per_unit - 1)
            def _():
                share(lax.div(done, per_unit))

        late = done - LATE

        @pl.when((late >= 0) & (lax.rem(late, per_group) == per_group - 1))
        def _():
            @pl.when(late < chunks - per_group)
            def _():
                steep_second(lax.div(late, per_group))

    each(end - LATE, step)

    for v in range(units):
        n_copy(v).wait_recv()
        field = n_twin[v].reshape(TILE * block, z_cells)
        dz[1, v] = from_right(field, tz_ref[...]).reshape(TILE, block, z_cells)
    for w in range(2 * units):
        for k in range(1, grids):
            gather_copy(w, k).wait_recv()
    along_first(0)
    nx[...] = turned(hx[...])
    for v in range(units):
        nx_copy(v).start()
    steps_done = [
        g for g in range(groups) if (g + 1) * per_group - 1 + LATE + slow - 1 < end - LATE
    ]
    done_groups = len([g for g in steps_done if (g + 1) * per_group - 1 < chunks - per_group])
    for g in range(done_groups, groups):
        steep_second(g)

    def potential_rows(v, e):
        span = pl.ds(e, XC_ROWS)
        here = pl.ds((2 * v + spin) * TILE + e, XC_ROWS)
        n_own, n_other = own[here], n_twin[v, span]
        g_own = [nx[here], ny[0, v, span], dz[0, v, span]]
        g_other = [nx_twin[v, span], ny[1, v, span], dz[1, v, span]]
        s_own = g_own[0] * g_own[0] + g_own[1] * g_own[1] + g_own[2] * g_own[2]
        s_mix = g_own[0] * g_other[0] + g_own[1] * g_other[1] + g_own[2] * g_other[2]
        s_other = g_other[0] * g_other[0] + g_other[1] * g_other[1] + g_other[2] * g_other[2]
        energy, pull = jax.vjp(xc_energy, n_own, n_other, s_own, s_mix, s_other)
        derivs = pull(jnp.ones_like(energy))
        base[here] = derivs[0]
        s_out[v, span] = derivs[1]
        flux = [
            [2.0 * derivs[2] * g_own[a] + derivs[3] * g_other[a] for a in range(3)],
            [2.0 * derivs[4] * g_other[a] + derivs[3] * g_own[a] for a in range(3)],
        ]
        for slot in range(2):
            fx[slot, span] = flux[slot][0]
            fy[slot, v, span] = flux[slot][1]
            fz[slot, span] = flux[slot][2]
        for r in range(XC_ROWS):
            row = (2 * v + spin) * TILE + e + r
            i, q = lax.div(row, bands), lax.rem(row, bands)
            fy_cross(v, e + r, i, q).start()

            @pl.when(q != me)
            def _():
                fy_own(v, e + r, i, q).start()

            @pl.when(q == me)
            def _():
                gy[1, i, my_block] = fy[0, v, e + r]

    def evaluate(v):
        for e in range(TILE):
            row = (2 * v + spin) * TILE + e

            @pl.when(lax.rem(row, bands) != me)
            def _():
                take(ny.at[0, v, e], yb_recv.at[0, v, e])

            take(ny.at[1, v, e], yb_recv.at[1, v, e])
        nx_copy(v).wait_recv()
        each(TILE // XC_ROWS, lambda e: potential_rows(v, e * XC_ROWS))
        gx[1, :, line_rows(2 * v + spin)] = turned(fx[0])
        fx_out[v] = turned(fx[1])
        for k in range(grids):
            if k > 0:
                fx_same(v, k).start()
            fx_cross(v, k).start()
        for slot in range(2):
            field = fz[slot].reshape(TILE * block, z_cells)
            slope = from_right(field, tz_ref[...]).reshape(TILE, block, z_cells)
            if slot == 0:
                mine = unit_rows(2 * v + spin)
                base[mine] = base[mine] - slope
            else:
                s_out[v] = s_out[v] - slope
        s_copy(v).start()

    def flux_second(i):
        take(gy.at[1, i, pl.ds(0, (bands - 1) * block)], fy_recv.at[i, 0])
        row, holder, v, e = my_row(i)

        @pl.when(holder != spin)
        def _():
            take(gy.at[1, i, pl.ds(0, block)], fy_recv.at[i, 1])

        hy[1, i] = from_left(ty_ref[...], gy[1, i])
        for k in range(1, bands):
            sb_copy(i, k).start()
        sy[row] = hy[1, i, my_block]

    def unit_step(v):
        evaluate(v)

        @pl.when(v >= 1)
        def _():
            each(pair_groups, lambda g: flux_second((v - 1) * pair_groups + g))

    each(units, unit_step)
    each(pair_groups, lambda g: flux_second((units - 1) * pair_groups + g))

    for v in range(units):
        for k in range(grids):
            if k > 0:
                fx_same(v, k).wait_recv()
            fx_cross(v, k).wait_recv()
    along_first(1)
    for v in range(units):
        s_copy(v).wait_recv()
    base[...] = base[...] - turned(hx[...])

    take(part.at[0], x_send)
    take(z_out.at[pl.ds(0, slow - 1)], z_send)
    take(own.at[pl.ds(0, rows - groups)], yf_send)
    take(sy.at[pl.ds(0, groups * (bands - 1))], yb_send)
    for g in range(groups):
        row, holder, v, e = my_row(g)

        @pl.when(holder != spin)
        def _():
            take(sy.at[0], yb_twin.at[g])

    take(fy.at[1], fy_other)

    def drain(v):
        n_copy(v).wait_send()
        nx_copy(v).wait_send()
        s_copy(v).wait_send()
        for k in range(grids):
            if k > 0:
                fx_same(v, k).wait_send()
                gather_copy(2 * v, k).wait_send()
                gather_copy(2 * v + 1, k).wait_send()
            fx_cross(v, k).wait_send()
        for e in range(TILE):
            row = (2 * v + spin) * TILE + e

            @pl.when(lax.rem(row, bands) != me)
            def _():
                take(fy.at[0, v, e], fy_send.at[v, e])

    each(units, drain)

    def finish(i):
        take(sy.at[pl.ds(0, bands - 1)], sb_recv.at[i])
        span = pl.ds(i * bands, bands)
        out_ref[span] = base[span] - sy[span]

    each(groups, finish)
    take(sy.at[pl.ds(0, groups * (bands - 1))], sb_send)


def potential_call(orbitals, partial_bands, core_density, tables):
    bands, grids = lax.axis_size("band"), lax.axis_size("grid")
    _, count, rows, y_cells, z_cells = orbitals.shape
    block, slow = y_cells // bands, bands // FAST
    x_cells = rows * grids
    chunk = min(CHUNK, TILE)
    chunks = rows // chunk
    units, groups = rows // (2 * TILE), rows // bands
    vmem = pl.BlockSpec(memory_space=pltpu.VMEM)
    hbm = pl.BlockSpec(memory_space=pl.ANY)
    dma = pltpu.SemaphoreType.DMA
    real = jnp.float32

    def held(*shape):
        return pltpu.VMEM(shape + (z_cells,), real)

    return pl.pallas_call(
        functools.partial(potential_kernel, bands, grids),
        out_shape=jax.ShapeDtypeStruct((rows, block, z_cells), real),
        in_specs=[pl.BlockSpec(memory_space=pltpu.SMEM), hbm, hbm] + [vmem] * 3,
        out_specs=vmem,
        scratch_shapes=[
            pltpu.VMEM((count, rows, y_cells, z_cells), jnp.bfloat16),
            held(rows, block),
            held(FAST, slow, rows, block),
            held(slow, rows, block),
            held(slow, rows, block),
            held(slow + 1, rows, block),
            held(rows, block),
            held(2, block, x_cells),
            held(block, rows),
            held(rows, block),
            held(2, groups, y_cells),
            held(2, groups, y_cells),
            held(2, units, TILE, block),
            held(2, units, TILE, block),
            held(units, TILE, block),
            held(units, TILE, block),
            held(2, TILE, block),
            held(units, block, TILE),
            held(2, units, TILE, block),
            held(2, TILE, block),
            held(units, TILE, block),
            held(rows, block),
            held(rows, block),
            dma((chunks,)),
            dma,
            dma,
            dma((chunks,)),
            dma,
            dma((chunks, slow + 1)),
            dma((2 * units, grids - 1)),
            dma((2 * units, grids - 1)),
            dma((units,)),
            dma((units,)),
            dma((units,)),
            dma((units,)),
            dma,
            dma((groups,)),
            dma,
            dma((groups,)),
            dma((2, units, TILE)),
            dma((units, TILE)),
            dma,
            dma((groups, 2)),
            dma((2, units, grids)),
            dma((2, units, grids)),
            dma((units,)),
            dma((units,)),
            dma,
            dma((groups,)),
        ],
        compiler_params=pltpu.CompilerParams(
            collective_id=0, has_side_effects=True, vmem_limit_bytes=60 * 2**20
        ),
        name="potential",
    )(partial_bands, orbitals, core_density, *tables)


def per_device(orbitals, partial_bands, core_density):
    rows, y_cells, z_cells = core_density.shape
    grids = lax.axis_size("grid")
    table = spectral_table(rows * grids)
    slabs = [left_table(table[g * rows : (g + 1) * rows]) for g in range(grids)]
    tables = (
        jnp.asarray(np.stack(slabs)),
        jnp.asarray(left_table(spectral_table(y_cells))),
        jnp.asarray(right_table(spectral_table(z_cells).T)),
    )
    return potential_call(orbitals, partial_bands, core_density, tables)[None]


def solution(mesh):
    in_specs = (P("spin", "band", "grid", None, None), P("spin", None), P("grid", None, None))
    out_specs = P("spin", "grid", "band", None)
    return jax.shard_map(
        per_device, mesh=mesh, in_specs=in_specs, out_specs=out_specs, check_vma=False
    )
```

time: 115 us -> 107 us (0.930)
  Pallas kernels: 113 us -> 105 us
    pallas_call x1, Pallas kernels: 113 us -> 105 us  [potential_call(): pl.pallas_call(functools.partial(potential_kernel, bands, grids), out_sha...]
where the time goes in v1:
time: 107 us; the launch traced here: 106 us
  Pallas kernels  105 us (98%)
  local copies, waits for them, and re-layouts  1.87 us (2%)
    pallas_call x1, Pallas kernels, potential_call(): pl.pallas_call(functools.partial(potential_kernel, bands, grids), out_sha...  105 us

profile of v1, /device:TPU:0, one launch (start us, length us, event | category | flops | bytes accessed | tf_op | source)
XLA Modules:
  0.0 106.4 jit_solution(17435565574826085123)
XLA Ops:
  0.0 104.6 %potential.1 = f32[64,16,128]{2,1,0:T(8,128)} custom-call(s32[1,2]{1,0:T(1,128)} %pairs_ref.1, bf16[1,8,64,128,128]{4,3,2,1,0:T(8,128)(2,1)} %orb_hbm.1, f32[64,128,128]{2,1,0:T(8,128)} %core_hbm.1, bf16[2,128,256]{2,1,0:T(8,128)(2,1)} %constant.6.clone.tx_ref, bf16[256,256]{1,0:T(8,128)(2,1)} %constant.7.clone.ty_ref, bf16[256,256]{1,0:T(8,128)(2,1)} %constant.8.clone.tz_ref), custom_call_target="tpu_custom_call" | custom-call | tf_op jit(solution)/shard_map/potential/pallas_call | solution.py:684
  104.6 1.9 %copy.8 = f32[1,64,16,128]{3,2,1,0:T(8,128)} copy(f32[1,64,16,128]{3,2,1,0:T(8,128)} %bitcast.1) | data formatting | bytes 1048576

commit v2 on v1

--- a/solution.py
+++ b/solution.py
@@ -19,6 +19,12 @@
 CHUNK = 4
 AHEAD = 3
 LATE = 2
+AFTER = 1
+BEHIND = 3
+FIRSTS = 2
+FIRST_STEP = 2
+FIRST_LAG = 1
+FIRST_LATE = 3
 FAST = 2
 XC_ROWS = 2
 TILE = 8
@@ -137,9 +143,9 @@
     pairs_ref,
     orb_hbm,
     core_hbm,
-    tx_ref,
-    ty_ref,
-    tz_ref,
+    tx_hbm,
+    ty_hbm,
+    tz_hbm,
     out_ref,
     orb,
     core,
@@ -147,6 +153,11 @@
     x_in,
     z_out,
     z_in,
+    f_in,
+    fx_in,
+    tx,
+    ty,
+    tz,
     own,
     gx,
     hx,
@@ -170,6 +181,14 @@
     x_recv,
     z_send,
     z_recv,
+    f_send,
+    f_recv,
+    fe_send,
+    fe_recv,
+    table_sem,
+    out_sem,
+    line_sem,
+    across_sem,
     g_send,
     g_recv,
     n_send,
@@ -194,8 +213,10 @@
     count, rows, y_cells, z_cells = orb.shape
     block = core.shape[1]
     slow = bands // FAST
+    stages = slow.bit_length() - 1
     chunk = x_in.shape[1] // x_recv.shape[0]
     chunks = rows // chunk
+    firsts = fe_recv.shape[0] if chunks >= 8 else 0
     per_unit = TILE // chunk
     units = rows // (2 * TILE)
     groups = rows // bands
@@ -205,6 +226,13 @@
     slab = lax.axis_index("grid")
     spin = lax.axis_index("spin")
     place, fast = lax.div(me, FAST), lax.rem(me, FAST)
+    bits = [lax.rem(lax.div(place, 2**k), 2) for k in range(stages)]
+    start, ranges = 0, []
+    for k in range(stages):
+        size = slow >> (k + 1)
+        ranges.append((size, start + bits[k] * size, start + (1 - bits[k]) * size))
+        start = start + bits[k] * size
+    spot = start
     across = {"band": place * FAST + (1 - fast)}
     twin = {"spin": 1 - spin}
     my_block = pl.ds(pl.multiple_of(me * block, TILE), block)
@@ -251,15 +279,50 @@
         span = chunk_span(c)
         return remote(part.at[1 - fast, :, span], x_in.at[:, span], x_send, x_recv.at[c], across)
 
-    def z_copy(c, d, slot, to):
+    def stage_peer(k):
+        return {"band": (place + (1 - 2 * bits[k]) * 2**k) * FAST + fast}
+
+    def stage_room(k):
+        size = ranges[k][0]
+        return pl.ds(slow - 2 * size, size)
+
+    def z_copy(c, k):
         span = chunk_span(c)
-        return remote(
-            z_out.at[d, span],
-            z_in.at[slot, span],
+        size, keep, give = ranges[k]
+        return remote(
+            z_out.at[pl.ds(give, size), span],
+            z_in.at[stage_room(k), span],
             z_send,
-            z_recv.at[c, slot],
-            {"band": to * FAST + fast},
-        )
+            z_recv.at[c, k],
+            stage_peer(k),
+        )
+
+    def f_copy(n, k):
+        size, keep, give = ranges[k]
+        return remote(
+            part.at[:, pl.ds(give, size), chunk_span(n)],
+            f_in.at[n, :, stage_room(k)],
+            f_send,
+            f_recv.at[n, k],
+            stage_peer(k),
+        )
+
+    def fe_copy(n):
+        return remote(
+            part.at[1 - fast, spot, chunk_span(n)],
+            fx_in.at[n],
+            fe_send.at[n],
+            fe_recv.at[n],
+            across,
+        )
+
+    def out_copy(i):
+        span = pl.ds(i * bands, bands)
+        return pltpu.make_async_copy(base.at[span], out_ref.at[span], out_sem.at[i])
+
+    def table_copy(t):
+        src, dst = [(tx_hbm, tx), (ty_hbm, ty), (tz_hbm, tz)][t]
+        return pltpu.make_async_copy(src, dst, table_sem.at[t])
 
     def gather_copy(w, k):
         return remote(
@@ -349,19 +412,60 @@
 
     each(chunks, lambda c: orb_copy(c).start())
     core_copy().start()
+    for t in range(3):
+        table_copy(t).start()
     barrier = pltpu.get_barrier_semaphore()
-    partners = [{"spin": 1 - spin}]
-    for core_id in (spin, 1 - spin):
-        partners += [{"spin": core_id, "band": lax.rem(me + k, bands)} for k in range(1, bands)]
-        partners += [{"spin": core_id, "grid": lax.rem(slab + k, grids)} for k in range(1, grids)]
+    beside = [(place > 0, place - 1), (place < slow - 1, place + 1)]
+    partners = [twin, across] + [{"grid": lax.rem(slab + k, grids)} for k in range(1, grids)]
     for target in partners:
         pl.semaphore_signal(barrier, inc=1, device_id=target, device_id_type=MESH)
+    for there, where in beside:
+
+        @pl.when(there)
+        def _():
+            pl.semaphore_signal(
+                barrier, inc=1, device_id={"band": where * FAST + fast}, device_id_type=MESH
+            )
+
+    neighbours = len(partners) + jnp.where(place > 0, 1, 0) + jnp.where(place < slow - 1, 1, 0)
+
+    turns = slow - 1
+
+    def call_on(turn):
+        if turn == turns - 1:
+            pl.semaphore_signal(across_sem, inc=1, device_id=across, device_id_type=MESH)
+            return
+        for side, (there, where) in enumerate(beside):
+
+            @pl.when(there)
+            def _():
+                pl.semaphore_signal(
+                    line_sem.at[turn, 1 - side],
+                    inc=1,
+                    device_id={"band": where * FAST + fast},
+                    device_id_type=MESH,
+                )
+
+    def hear(turn):
+        if turn == turns - 1:
+            pl.semaphore_wait(across_sem, 1)
+            return
+        for side, (there, where) in enumerate(beside):
+
+            @pl.when(there)
+            def _():
+                pl.semaphore_wait(line_sem.at[turn, side], 1)
+
+        call_on(turn + 1)
+
     first = pairs_ref[0, 0]
     last = first + pairs_ref[0, 1]
     weights = []
     for n in range(count):
         ident = me * count + n
         weights.append(jnp.where((ident >= first) & (ident < last), 0.5, 1.0).astype(jnp.float32))
+
+    reverse = [sum((d >> k & 1) << (stages - 1 - k) for k in range(stages)) for d in range(slow)]
 
     def squares(c):
         orb_copy(c).wait()
@@ -372,49 +476,41 @@
                 for n in range(count):
                     values = orb[n, row, b * block : (b + 1) * block].astype(jnp.float32)
                     total += weights[n] * (values * values)
-                part[b % FAST, b // FAST, row] = total
+                part[b % FAST, reverse[b // FAST], row] = total
 
     def sum_across(c):
         x_copy(c).wait_recv()
         span = chunk_span(c)
-        for d in range(slow):
-            z_out[d, span] = part[fast, d, span] + x_in[d, span]
-
-        @pl.when(place == 0)
-        def _():
-            for d in range(slow - 1, 0, -1):
-                z_copy(c, d, d, 1).start()
-
-        @pl.when(place == slow - 1)
-        def _():
-            for d in range(slow - 1):
-                z_copy(c, d, slow if d == slow - 2 else d, slow - 2).start()
-
-    def hop(h, c):
+        z_out[:, span] = part[fast, :, span] + x_in[:, span]
+        z_copy(c, 0).start()
+
+    def stage(k, c):
         span = chunk_span(c)
-
-        @pl.when(place == h)
-        def _():
-            for d in range(slow - 1, h - 1, -1):
-                z_copy(c, d, d, h).wait_recv()
-                z_out[d, span] += z_in[d, span]
-                if d > h:
-                    z_copy(c, d, d, h + 1).start()
-
-        at = slow - 1 - h
-
-        @pl.when(place == at)
-        def _():
-            for d in range(at + 1):
-                slot = slow if d == at else d
-                z_copy(c, d, slot, at).wait_recv()
-                z_out[d, span] += z_in[slot, span]
-                if d < at:
-                    z_copy(c, d, slow if d == at - 1 else d, at - 1).start()
-
-    def collect(c):
+        z_copy(c, k).wait_recv()
+        size, keep, give = ranges[k]
+        z_out[pl.ds(keep, size), span] += z_in[stage_room(k), span]
+        if k + 1 < stages:
+            z_copy(c, k + 1).start()
+
+    def first_stage(k, n):
+        span = chunk_span(n)
+        f_copy(n, k).wait_recv()
+        size, keep, give = ranges[k]
+        part[:, pl.ds(keep, size), span] += f_in[n, :, stage_room(k)]
+        if k + 1 < stages:
+            f_copy(n, k + 1).start()
+        else:
+            fe_copy(n).start()
+
+    def first_end(n):
+        fe_copy(n).wait_recv()
+        collect(n, part[fast, spot, chunk_span(n)] + fx_in[n])
+        if (n + 1) % per_unit == 0:
+            share(n // per_unit)
+
+    def collect(c, total):
         span = chunk_span(c)
-        own[span] = 0.5 * core[span] + z_out[place, span]
+        own[span] = 0.5 * core[span] + total
         for r in range(chunk):
             row = c * chunk + r
             i, q = lax.div(row, bands), lax.rem(row, bands)
@@ -442,11 +538,11 @@
         @pl.when(lax.rem(w, 2) == spin)
         def _():
             field = own[unit_rows(w)].reshape(TILE * block, z_cells)
-            dz[0, v] = from_right(field, tz_ref[...]).reshape(TILE, block, z_cells)
+            dz[0, v] = from_right(field, tz[...]).reshape(TILE, block, z_cells)
 
     def steep_second(i):
         take(gy.at[0, i, pl.ds(0, (bands - 1) * block)], yf_recv.at[i])
-        hy[0, i] = from_left(ty_ref[...], gy[0, i])
+        hy[0, i] = from_left(ty[...], gy[0, i])
         for k in range(1, bands):
             yb_copy(i, lax.rem(me + k, bands), yb_send).start()
         row, holder, v, e = my_row(i)
@@ -460,7 +556,7 @@
             yb_copy(i, me, yb_twin.at[i]).start()
 
     def along_first(t):
-        table = tx_ref[slab]
+        table = tx[slab]
         for y in range(0, block, 2):
             pair = jnp.concatenate([gx[t, y], gx[t, y + 1]], axis=1)
             product = from_left(table, pair)
@@ -468,54 +564,95 @@
             hx[y + 1] = product[:, z_cells:]
 
     ahead = min(AHEAD, chunks)
-    for c in range(ahead):
+    left = chunks - firsts
+    order = [firsts] + [c for n in range(1, ahead) for c in (n - 1, firsts + n) if c != n - 1 or n <= firsts]
+    order += list(range(ahead - 1, firsts))
+    for at, c in enumerate(order):
         squares(c)
-        if c == 0:
-            pl.semaphore_wait(barrier, len(partners))
-        x_copy(c).start()
-    core_copy().wait()
-    end = chunks + slow - 1 + LATE
+        if at == 0:
+            pl.semaphore_wait(barrier, neighbours)
+        if c < firsts:
+            f_copy(c, 0).start()
+        else:
+            x_copy(c).start()
+    call_on(0)
+    end = left + stages
+    inside = max(min((chunks - LATE) // per_group, groups - AFTER), 0)
+    first_groups = firsts // per_group
+    finish_first = FIRST_STEP * stages + ahead + FIRST_LAG
 
     def step(u):
-        @pl.when(u + ahead < chunks)
-        def _():
-            squares(u + ahead)
-            x_copy(u + ahead).start()
-
-        @pl.when(u < chunks)
-        def _():
-            sum_across(u)
-
-        for h in range(1, slow):
-
-            @pl.when((u >= h) & (u < chunks + h))
-            def _():
-                hop(h, u - h)
-
-        done = u - (slow - 1)
-
-        @pl.when((done >= 0) & (done < chunks))
-        def _():
-            collect(done)
-
-            @pl.when(lax.rem(done, per_unit) == per_unit - 1)
-            def _():
-                share(lax.div(done, per_unit))
-
-        late = done - LATE
-
-        @pl.when((late >= 0) & (lax.rem(late, per_group) == per_group - 1))
-        def _():
-            @pl.when(late < chunks - per_group)
-            def _():
-                steep_second(lax.div(late, per_group))
-
-    each(end - LATE, step)
+        @pl.when(u + ahead < left)
+        def _():
+            squares(firsts + u + ahead)
+            x_copy(firsts + u + ahead).start()
+
+        @pl.when(u < left)
+        def _():
+            sum_across(firsts + u)
+
+        for turn in range(turns):
+
+            @pl.when(u == min(turn, stages))
+            def _():
+                hear(turn)
+
+        for k in range(stages):
+
+            @pl.when((u > k) & (u < left + k + 1))
+            def _():
+                stage(k, firsts + u - k - 1)
+
+        @pl.when(u == stages)
+        def _():
+            core_copy().wait()
+            for t in range(3):
+                table_copy(t).wait()
+
+        done = u - stages
+
+        @pl.when((done >= 0) & (done < left))
+        def _():
+            c = firsts + done
+            collect(c, z_out[spot, chunk_span(c)])
+
+            @pl.when(lax.rem(c, per_unit) == per_unit - 1)
+            def _():
+                share(lax.div(c, per_unit))
+
+        for n in range(firsts):
+            for k in range(stages):
+
+                @pl.when(u == 1 + FIRST_STEP * k + n)
+                def _():
+                    first_stage(k, n)
+
+            @pl.when(u == finish_first + n)
+            def _():
+                first_end(n)
+
+        for g in range(first_groups):
+
+            @pl.when(u == finish_first + (g + 1) * per_group - 1 + FIRST_LATE)
+            def _():
+                steep_second(g)
+
+        late = firsts + done - LATE
+
+        @pl.when(
+            (late >= firsts)
+            & (late < inside * per_group)
+            & (lax.rem(late, per_group) == per_group - 1)
+        )
+        def _():
+            steep_second(lax.div(late, per_group))
+
+    each(end, step)
 
     for v in range(units):
         n_copy(v).wait_recv()
         field = n_twin[v].reshape(TILE * block, z_cells)
-        dz[1, v] = from_right(field, tz_ref[...]).reshape(TILE, block, z_cells)
+        dz[1, v] = from_right(field, tz[...]).reshape(TILE, block, z_cells)
     for w in range(2 * units):
         for k in range(1, grids):
             gather_copy(w, k).wait_recv()
@@ -523,12 +660,7 @@
     nx[...] = turned(hx[...])
     for v in range(units):
         nx_copy(v).start()
-    steps_done = [
-        g for g in range(groups) if (g + 1) * per_group - 1 + LATE + slow - 1 < end - LATE
-    ]
-    done_groups = len([g for g in steps_done if (g + 1) * per_group - 1 < chunks - per_group])
-    for g in range(done_groups, groups):
-        steep_second(g)
+    each(groups - inside, lambda g: steep_second(inside + g))
 
     def potential_rows(v, e):
         span = pl.ds(e, XC_ROWS)
@@ -583,7 +715,7 @@
             fx_cross(v, k).start()
         for slot in range(2):
             field = fz[slot].reshape(TILE * block, z_cells)
-            slope = from_right(field, tz_ref[...]).reshape(TILE, block, z_cells)
+            slope = from_right(field, tz[...]).reshape(TILE, block, z_cells)
             if slot == 0:
                 mine = unit_rows(2 * v + spin)
                 base[mine] = base[mine] - slope
@@ -599,7 +731,7 @@
         def _():
             take(gy.at[1, i, pl.ds(0, block)], fy_recv.at[i, 1])
 
-        hy[1, i] = from_left(ty_ref[...], gy[1, i])
+        hy[1, i] = from_left(ty[...], gy[1, i])
         for k in range(1, bands):
             sb_copy(i, k).start()
         sy[row] = hy[1, i, my_block]
@@ -607,12 +739,13 @@
     def unit_step(v):
         evaluate(v)
 
-        @pl.when(v >= 1)
-        def _():
-            each(pair_groups, lambda g: flux_second((v - 1) * pair_groups + g))
+        @pl.when(v >= BEHIND)
+        def _():
+            each(pair_groups, lambda g: flux_second((v - BEHIND) * pair_groups + g))
 
     each(units, unit_step)
-    each(pair_groups, lambda g: flux_second((units - 1) * pair_groups + g))
+    behind = min(BEHIND, units) * pair_groups
+    each(behind, lambda g: flux_second(groups - behind + g))
 
     for v in range(units):
         for k in range(grids):
@@ -624,8 +757,12 @@
         s_copy(v).wait_recv()
     base[...] = base[...] - turned(hx[...])
 
-    take(part.at[0], x_send)
-    take(z_out.at[pl.ds(0, slow - 1)], z_send)
+    take(part.at[0, :, pl.ds(0, left * chunk)], x_send)
+    take(z_out.at[pl.ds(0, slow - 1), pl.ds(0, left * chunk)], z_send)
+    if firsts:
+        take(part.at[:, pl.ds(0, slow - 1), pl.ds(0, firsts * chunk)], f_send)
+    for n in range(firsts):
+        fe_copy(n).wait_send()
     take(own.at[pl.ds(0, rows - groups)], yf_send)
     take(sy.at[pl.ds(0, groups * (bands - 1))], yb_send)
     for g in range(groups):
@@ -659,9 +796,11 @@
     def finish(i):
         take(sy.at[pl.ds(0, bands - 1)], sb_recv.at[i])
         span = pl.ds(i * bands, bands)
-        out_ref[span] = base[span] - sy[span]
+        base[span] = base[span] - sy[span]
+        out_copy(i).start()
 
     each(groups, finish)
+    each(groups, lambda i: out_copy(i).wait())
     take(sy.at[pl.ds(0, groups * (bands - 1))], sb_send)
 
 
@@ -669,11 +808,11 @@
     bands, grids = lax.axis_size("band"), lax.axis_size("grid")
     _, count, rows, y_cells, z_cells = orbitals.shape
     block, slow = y_cells // bands, bands // FAST
+    stages = slow.bit_length() - 1
     x_cells = rows * grids
     chunk = min(CHUNK, TILE)
     chunks = rows // chunk
     units, groups = rows // (2 * TILE), rows // bands
-    vmem = pl.BlockSpec(memory_space=pltpu.VMEM)
     hbm = pl.BlockSpec(memory_space=pl.ANY)
     dma = pltpu.SemaphoreType.DMA
     real = jnp.float32
@@ -684,15 +823,18 @@
     return pl.pallas_call(
         functools.partial(potential_kernel, bands, grids),
         out_shape=jax.ShapeDtypeStruct((rows, block, z_cells), real),
-        in_specs=[pl.BlockSpec(memory_space=pltpu.SMEM), hbm, hbm] + [vmem] * 3,
-        out_specs=vmem,
+        in_specs=[pl.BlockSpec(memory_space=pltpu.SMEM)] + [hbm] * 5,
+        out_specs=hbm,
         scratch_shapes=[
             pltpu.VMEM((count, rows, y_cells, z_cells), jnp.bfloat16),
             held(rows, block),
             held(FAST, slow, rows, block),
             held(slow, rows, block),
             held(slow, rows, block),
-            held(slow + 1, rows, block),
+            held(slow - 1, rows, block),
+            held(FIRSTS, FAST, slow - 1, chunk, block),
+            held(FIRSTS, chunk, block),
+            *[pltpu.VMEM(table.shape, table.dtype) for table in tables],
             held(rows, block),
             held(2, block, x_cells),
             held(block, rows),
@@ -715,7 +857,15 @@
             dma,
             dma((chunks,)),
             dma,
-            dma((chunks, slow + 1)),
+            dma((chunks, stages)),
+            dma,
+            dma((FIRSTS, stages)),
+            dma((FIRSTS,)),
+            dma((FIRSTS,)),
+            dma((3,)),
+            dma((groups,)),
+            pltpu.SemaphoreType.REGULAR((max(slow - 2, 1), 2)),
+            pltpu.SemaphoreType.REGULAR,
             dma((2 * units, grids - 1)),
             dma((2 * units, grids - 1)),
             dma((units,)),

time: 107 us -> 102 us (0.953)
  Pallas kernels: 105 us -> 100 us
    pallas_call x1, Pallas kernels: 105 us -> 100 us  [potential_call(): pl.pallas_call(functools.partial(potential_kernel, bands, grids), out_sha...]
where the time goes in v2:
time: 102 us
  Pallas kernels  100 us (98%)
  local copies, waits for them, and re-layouts  1.87 us (2%)
    pallas_call x1, Pallas kernels, potential_call(): pl.pallas_call(functools.partial(potential_kernel, bands, grids), out_sha...  100 us

profile of v2, /device:TPU:0, one launch (start us, length us, event | category | flops | bytes accessed | tf_op | source)
XLA Modules:
  0.0 102.0 jit_solution(5985276339528294204)
XLA Ops:
  0.0 100.2 %potential.1 = f32[64,16,128]{2,1,0:T(8,128)} custom-call(s32[1,2]{1,0:T(1,128)} %pairs_ref.1, bf16[1,8,64,128,128]{4,3,2,1,0:T(8,128)(2,1)} %orb_hbm.1, f32[64,128,128]{2,1,0:T(8,128)} %core_hbm.1, bf16[2,128,256]{2,1,0:T(8,128)(2,1)} %constant.6.clone.tx_hbm, bf16[256,256]{1,0:T(8,128)(2,1)} %constant.7.clone.ty_hbm, bf16[256,256]{1,0:T(8,128)(2,1)} %constant.8.clone.tz_hbm), custom_call_target="tpu_custom_call" | custom-call | tf_op jit(solution)/shard_map/potential/pallas_call | solution.py:823
  100.2 1.9 %copy.8 = f32[1,64,16,128]{3,2,1,0:T(8,128)} copy(f32[1,64,16,128]{3,2,1,0:T(8,128)} %bitcast.1) | data formatting | bytes 1048576

commit v3 on v2

--- a/solution.py
+++ b/solution.py
@@ -23,7 +23,8 @@
 BEHIND = 3
 FIRSTS = 2
 FIRST_STEP = 2
-FIRST_LAG = 1
+FIRST_LAG = 3
+DEPTH = 6
 FIRST_LATE = 3
 FAST = 2
 XC_ROWS = 2
@@ -218,6 +219,7 @@
     chunks = rows // chunk
     firsts = fe_recv.shape[0] if chunks >= 8 else 0
     per_unit = TILE // chunk
+    depth = orb_sem.shape[0]
     units = rows // (2 * TILE)
     groups = rows // bands
     per_group = bands // chunk
@@ -250,6 +252,22 @@
     def take(ref, sem):
         pltpu.make_async_copy(ref, ref, sem).wait()
 
+    mine = True if bands == TILE else lax.rem(lax.div(me, TILE), 2) == spin
+
+    def take_rows(ref, ones, sem):
+        full = ref.shape[0]
+        if bands == TILE:
+            take(ref.at[pl.ds(0, full - ones)], sem)
+        else:
+
+            @pl.when(mine)
+            def _():
+                take(ref.at[pl.ds(0, full - ones)], sem)
+
+            @pl.when(jnp.logical_not(mine))
+            def _():
+                take(ref, sem)
+
     def each(number, body):
         lax.fori_loop(0, number, lambda i, carry: (body(i), carry)[1], 0)
 
@@ -270,7 +288,7 @@
 
     def orb_copy(c):
         span = chunk_span(c)
-        return pltpu.make_async_copy(orb_hbm.at[0, :, span], orb.at[:, span], orb_sem.at[c])
+        return pltpu.make_async_copy(orb_hbm.at[0, :, span], orb.at[:, span], orb_sem.at[lax.rem(c, depth)])
 
     def core_copy():
         return pltpu.make_async_copy(core_hbm.at[:, my_block], core, core_sem)
@@ -318,7 +336,7 @@
 
     def out_copy(i):
         span = pl.ds(i * bands, bands)
-        return pltpu.make_async_copy(base.at[span], out_ref.at[span], out_sem.at[i])
+        return pltpu.make_async_copy(base.at[span], out_ref.at[span], out_sem)
 
     def table_copy(t):
         src, dst = [(tx_hbm, tx), (ty_hbm, ty), (tz_hbm, tz)][t]
@@ -328,27 +346,27 @@
         return remote(
             gx.at[0, :, line_rows(w)],
             gx.at[0, :, line_rows(w)],
-            g_send.at[w, k - 1],
-            g_recv.at[w, k - 1],
+            g_send,
+            g_recv,
             {"grid": lax.rem(slab + k, grids)},
         )
 
     def n_copy(v):
         return remote(
-            own.at[unit_rows(2 * v + 1 - spin)], n_twin.at[v], n_send.at[v], n_recv.at[v], twin
+            own.at[unit_rows(2 * v + 1 - spin)], n_twin.at[v], n_send, n_recv, twin
         )
 
     def nx_copy(v):
         return remote(
-            nx.at[unit_rows(2 * v + 1 - spin)], nx_twin.at[v], nx_send.at[v], nx_recv.at[v], twin
+            nx.at[unit_rows(2 * v + 1 - spin)], nx_twin.at[v], nx_send, nx_recv.at[v], twin
         )
 
     def fx_same(v, k):
         return remote(
             gx.at[1, :, line_rows(2 * v + spin)],
             gx.at[1, :, line_rows(2 * v + spin)],
-            fx_send.at[0, v, k],
-            fx_recv.at[0, v, k],
+            fx_send.at[0],
+            fx_recv,
             {"grid": lax.rem(slab + k, grids)},
         )
 
@@ -356,14 +374,14 @@
         return remote(
             fx_out.at[v],
             gx.at[1, :, line_rows(2 * v + spin)],
-            fx_send.at[1, v, k],
-            fx_recv.at[1, v, k],
+            fx_send.at[1],
+            fx_recv,
             {"spin": 1 - spin, "grid": lax.rem(slab + k, grids)},
         )
 
     def s_copy(v):
         return remote(
-            s_out.at[v], base.at[unit_rows(2 * v + spin)], s_send.at[v], s_recv.at[v], twin
+            s_out.at[v], base.at[unit_rows(2 * v + spin)], s_send, s_recv, twin
         )
 
     def my_row(i):
@@ -378,7 +396,7 @@
             hy.at[0, i, band_block(j)],
             ny.at[slot, v, e],
             send,
-            yb_recv.at[slot, v, e],
+            yb_recv.at[slot, v],
             {"spin": holder, "band": j},
         )
 
@@ -386,7 +404,7 @@
         return remote(
             fy.at[0, v, e],
             gy.at[1, i, my_block],
-            fy_send.at[v, e],
+            fy_send,
             fy_recv.at[i, 0],
             {"band": q},
         )
@@ -410,7 +428,7 @@
             {"band": q},
         )
 
-    each(chunks, lambda c: orb_copy(c).start())
+    each(depth, lambda c: orb_copy(c).start())
     core_copy().start()
     for t in range(3):
         table_copy(t).start()
@@ -478,6 +496,10 @@
                     total += weights[n] * (values * values)
                 part[b % FAST, reverse[b // FAST], row] = total
 
+        @pl.when(c + depth < chunks)
+        def _():
+            orb_copy(c + depth).start()
+
     def sum_across(c):
         x_copy(c).wait_recv()
         span = chunk_span(c)
@@ -553,7 +575,7 @@
 
         @pl.when(holder != spin)
         def _():
-            yb_copy(i, me, yb_twin.at[i]).start()
+            yb_copy(i, me, yb_twin).start()
 
     def along_first(t):
         table = tx[slab]
@@ -649,13 +671,11 @@
 
     each(end, step)
 
+    take(n_twin, n_recv)
     for v in range(units):
-        n_copy(v).wait_recv()
         field = n_twin[v].reshape(TILE * block, z_cells)
         dz[1, v] = from_right(field, tz[...]).reshape(TILE, block, z_cells)
-    for w in range(2 * units):
-        for k in range(1, grids):
-            gather_copy(w, k).wait_recv()
+    take(gx.at[0, :, pl.ds(0, (grids - 1) * rows)], g_recv)
     along_first(0)
     nx[...] = turned(hx[...])
     for v in range(units):
@@ -697,14 +717,8 @@
                 gy[1, i, my_block] = fy[0, v, e + r]
 
     def evaluate(v):
-        for e in range(TILE):
-            row = (2 * v + spin) * TILE + e
-
-            @pl.when(lax.rem(row, bands) != me)
-            def _():
-                take(ny.at[0, v, e], yb_recv.at[0, v, e])
-
-            take(ny.at[1, v, e], yb_recv.at[1, v, e])
+        take_rows(ny.at[0, v], 1, yb_recv.at[0, v])
+        take(ny.at[1, v], yb_recv.at[1, v])
         nx_copy(v).wait_recv()
         each(TILE // XC_ROWS, lambda e: potential_rows(v, e * XC_ROWS))
         gx[1, :, line_rows(2 * v + spin)] = turned(fx[0])
@@ -747,14 +761,9 @@
     behind = min(BEHIND, units) * pair_groups
     each(behind, lambda g: flux_second(groups - behind + g))
 
-    for v in range(units):
-        for k in range(grids):
-            if k > 0:
-                fx_same(v, k).wait_recv()
-            fx_cross(v, k).wait_recv()
+    take(gx.at[1, :, pl.ds(0, (2 * grids - 1) * units * TILE)], fx_recv)
     along_first(1)
-    for v in range(units):
-        s_copy(v).wait_recv()
+    take(s_out, s_recv)
     base[...] = base[...] - turned(hx[...])
 
     take(part.at[0, :, pl.ds(0, left * chunk)], x_send)
@@ -765,33 +774,22 @@
         fe_copy(n).wait_send()
     take(own.at[pl.ds(0, rows - groups)], yf_send)
     take(sy.at[pl.ds(0, groups * (bands - 1))], yb_send)
-    for g in range(groups):
-        row, holder, v, e = my_row(g)
-
-        @pl.when(holder != spin)
-        def _():
-            take(sy.at[0], yb_twin.at[g])
+    if bands == TILE:
+        take(sy.at[pl.ds(0, units)], yb_twin)
+    else:
+
+        @pl.when(jnp.logical_not(mine))
+        def _():
+            take(sy.at[pl.ds(0, groups)], yb_twin)
 
     take(fy.at[1], fy_other)
-
-    def drain(v):
-        n_copy(v).wait_send()
-        nx_copy(v).wait_send()
-        s_copy(v).wait_send()
-        for k in range(grids):
-            if k > 0:
-                fx_same(v, k).wait_send()
-                gather_copy(2 * v, k).wait_send()
-                gather_copy(2 * v + 1, k).wait_send()
-            fx_cross(v, k).wait_send()
-        for e in range(TILE):
-            row = (2 * v + spin) * TILE + e
-
-            @pl.when(lax.rem(row, bands) != me)
-            def _():
-                take(fy.at[0, v, e], fy_send.at[v, e])
-
-    each(units, drain)
+    take_rows(sy.at[pl.ds(0, units * TILE)], units, fy_send)
+    take(own.at[pl.ds(0, units * TILE)], n_send)
+    take(own.at[pl.ds(0, units * TILE)], nx_send)
+    take(s_out, s_send)
+    take(gx.at[0, :, pl.ds(0, (grids - 1) * rows)], g_send)
+    take(gx.at[1, :, pl.ds(0, (grids - 1) * units * TILE)], fx_send.at[0])
+    take(gx.at[1, :, pl.ds(0, grids * units * TILE)], fx_send.at[1])
 
     def finish(i):
         take(sy.at[pl.ds(0, bands - 1)], sb_recv.at[i])
@@ -800,7 +798,7 @@
         out_copy(i).start()
 
     each(groups, finish)
-    each(groups, lambda i: out_copy(i).wait())
+    take(base, out_sem)
     take(sy.at[pl.ds(0, groups * (bands - 1))], sb_send)
 
 
@@ -852,7 +850,7 @@
             held(units, TILE, block),
             held(rows, block),
             held(rows, block),
-            dma((chunks,)),
+            dma((min(DEPTH, chunks),)),
             dma,
             dma,
             dma((chunks,)),
@@ -863,27 +861,27 @@
             dma((FIRSTS,)),
             dma((FIRSTS,)),
             dma((3,)),
-            dma((groups,)),
+            dma,
             pltpu.SemaphoreType.REGULAR((max(slow - 2, 1), 2)),
             pltpu.SemaphoreType.REGULAR,
-            dma((2 * units, grids - 1)),
-            dma((2 * units, grids - 1)),
+            dma,
+            dma,
+            dma,
+            dma,
+            dma,
             dma((units,)),
-            dma((units,)),
-            dma((units,)),
-            dma((units,)),
             dma,
             dma((groups,)),
             dma,
-            dma((groups,)),
-            dma((2, units, TILE)),
-            dma((units, TILE)),
+            dma,
+            dma((2, units)),
+            dma,
             dma,
             dma((groups, 2)),
-            dma((2, units, grids)),
-            dma((2, units, grids)),
-            dma((units,)),
-            dma((units,)),
+            dma((2,)),
+            dma,
+            dma,
+            dma,
             dma,
             dma((groups,)),
         ],

time: 102 us -> 100 us (0.980)
  Pallas kernels: 100 us -> 98.1 us
    pallas_call x1, Pallas kernels: 100 us -> 98.1 us  [potential_call(): pl.pallas_call(functools.partial(potential_kernel, bands, grids), out_sha...]
where the time goes in v3:
time: 100 us
  Pallas kernels  98.1 us (98%)
  local copies, waits for them, and re-layouts  1.87 us (2%)
    pallas_call x1, Pallas kernels, potential_call(): pl.pallas_call(functools.partial(potential_kernel, bands, grids), out_sha...  98.1 us

profile of v3, /device:TPU:0, one launch (start us, length us, event | category | flops | bytes accessed | tf_op | source)
XLA Modules:
  0.0 100.0 jit_solution(12422255220329255169)
XLA Ops:
  0.0 98.1 %potential.1 = f32[64,16,128]{2,1,0:T(8,128)} custom-call(s32[1,2]{1,0:T(1,128)} %pairs_ref.1, bf16[1,8,64,128,128]{4,3,2,1,0:T(8,128)(2,1)} %orb_hbm.1, f32[64,128,128]{2,1,0:T(8,128)} %core_hbm.1, bf16[2,128,256]{2,1,0:T(8,128)(2,1)} %constant.6.clone.tx_hbm, bf16[256,256]{1,0:T(8,128)(2,1)} %constant.7.clone.ty_hbm, bf16[256,256]{1,0:T(8,128)(2,1)} %constant.8.clone.tz_hbm), custom_call_target="tpu_custom_call" | custom-call | tf_op jit(solution)/shard_map/potential/pallas_call | solution.py:821
  98.1 1.9 %copy.8 = f32[1,64,16,128]{3,2,1,0:T(8,128)} copy(f32[1,64,16,128]{3,2,1,0:T(8,128)} %bitcast.1) | data formatting | bytes 1048576

commit v4 on v3

--- a/solution.py
+++ b/solution.py
@@ -17,13 +17,13 @@
 FPP_ZERO = 1.709921
 MESH = pl.DeviceIdType.MESH
 CHUNK = 4
-AHEAD = 3
-LATE = 2
+AHEAD = 4
+LATE = 3
 AFTER = 1
 BEHIND = 3
 FIRSTS = 2
 FIRST_STEP = 2
-FIRST_LAG = 3
+FIRST_LAG = 2
 DEPTH = 6
 FIRST_LATE = 3
 FAST = 2
@@ -215,7 +215,7 @@
     block = core.shape[1]
     slow = bands // FAST
     stages = slow.bit_length() - 1
-    chunk = x_in.shape[1] // x_recv.shape[0]
+    chunk = min(CHUNK, TILE)
     chunks = rows // chunk
     firsts = fe_recv.shape[0] if chunks >= 8 else 0
     per_unit = TILE // chunk
@@ -295,7 +295,7 @@
 
     def x_copy(c):
         span = chunk_span(c)
-        return remote(part.at[1 - fast, :, span], x_in.at[:, span], x_send, x_recv.at[c], across)
+        return remote(part.at[1 - fast, :, span], x_in.at[:, span], x_send, x_recv.at[lax.rem(c, x_recv.shape[0])], across)
 
     def stage_peer(k):
         return {"band": (place + (1 - 2 * bits[k]) * 2**k) * FAST + fast}
@@ -311,7 +311,7 @@
             z_out.at[pl.ds(give, size), span],
             z_in.at[stage_room(k), span],
             z_send,
-            z_recv.at[c, k],
+            z_recv.at[lax.rem(c, z_recv.shape[0]), k],
             stage_peer(k),
         )
 
@@ -405,7 +405,7 @@
             fy.at[0, v, e],
             gy.at[1, i, my_block],
             fy_send,
-            fy_recv.at[i, 0],
+            fy_recv.at[i],
             {"band": q},
         )
 
@@ -414,7 +414,7 @@
             fy.at[1, v, e],
             gy.at[1, i, my_block],
             fy_other,
-            fy_recv.at[i, jnp.where(q == me, 1, 0)],
+            fy_recv.at[i],
             {"spin": 1 - spin, "band": q},
         )
 
@@ -738,12 +738,15 @@
         s_copy(v).start()
 
     def flux_second(i):
-        take(gy.at[1, i, pl.ds(0, (bands - 1) * block)], fy_recv.at[i, 0])
         row, holder, v, e = my_row(i)
 
+        @pl.when(holder == spin)
+        def _():
+            take(gy.at[1, i, pl.ds(0, (bands - 1) * block)], fy_recv.at[i])
+
         @pl.when(holder != spin)
         def _():
-            take(gy.at[1, i, pl.ds(0, block)], fy_recv.at[i, 1])
+            take(gy.at[1, i], fy_recv.at[i])
 
         hy[1, i] = from_left(ty[...], gy[1, i])
         for k in range(1, bands):
@@ -853,9 +856,9 @@
             dma((min(DEPTH, chunks),)),
             dma,
             dma,
-            dma((chunks,)),
-            dma,
-            dma((chunks, stages)),
+            dma((min(2 * AHEAD + 2, chunks),)),
+            dma,
+            dma((min(4, chunks), stages)),
             dma,
             dma((FIRSTS, stages)),
             dma((FIRSTS,)),
@@ -877,7 +880,7 @@
             dma((2, units)),
             dma,
             dma,
-            dma((groups, 2)),
+            dma((groups,)),
             dma((2,)),
             dma,
             dma,

time: 100 us -> 99.4 us (level)
  no operation moved by 1% of the time
where the time goes in v4:
time: 99.4 us; the launch traced here: 99.3 us
  Pallas kernels  97.4 us (98%)
  local copies, waits for them, and re-layouts  1.87 us (2%)
    pallas_call x1, Pallas kernels, potential_call(): pl.pallas_call(functools.partial(potential_kernel, bands, grids), out_sha...  97.4 us

profile of v4, /device:TPU:0, one launch (start us, length us, event | category | flops | bytes accessed | tf_op | source)
XLA Modules:
  0.0 99.3 jit_solution(3646852821666911502)
XLA Ops:
  0.0 97.4 %potential.1 = f32[64,16,128]{2,1,0:T(8,128)} custom-call(s32[1,2]{1,0:T(1,128)} %pairs_ref.1, bf16[1,8,64,128,128]{4,3,2,1,0:T(8,128)(2,1)} %orb_hbm.1, f32[64,128,128]{2,1,0:T(8,128)} %core_hbm.1, bf16[2,128,256]{2,1,0:T(8,128)(2,1)} %constant.6.clone.tx_hbm, bf16[256,256]{1,0:T(8,128)(2,1)} %constant.7.clone.ty_hbm, bf16[256,256]{1,0:T(8,128)(2,1)} %constant.8.clone.tz_hbm), custom_call_target="tpu_custom_call" | custom-call | tf_op jit(solution)/shard_map/potential/pallas_call | solution.py:824
  97.4 1.9 %copy.8 = f32[1,64,16,128]{3,2,1,0:T(8,128)} copy(f32[1,64,16,128]{3,2,1,0:T(8,128)} %bitcast.1) | data formatting | bytes 1048576
